TPU v7x, 256 devices: a whole 4x4x8 slice. The times are simulated.
256 devices in a mesh: gx: 8 (over y, core), gy: 2 (over x_hi), ta: 16 (over z, x_lo).
Axes of the slice: x: 4 (x_hi: 2, x_lo: 2; x = x_hi * 2 + x_lo), y: 4, z: 8, core: 2. Of those that a mesh axis runs over, the one named last changes fastest.
Arguments:
- link_x: float32 [2, 3, 3, 32, 64, 256], P(None, None, None, 'gx', 'ta', 'gy'), may hold values from -1 to 1, as said below
- link_t: float32 [2, 3, 3, 32, 64, 256], P(None, None, None, 'gx', 'ta', 'gy'), may hold values from -1 to 1, as said below
Outputs:
- loops: float32 [6, 6, 32, 64], P(None, None, 'gx', 'ta')
Inputs may be any that keep to these rules, and one draw needn't show every extreme that they name: `link_x`: every link matrix is special unitary. `link_t`: every link matrix is special unitary.
All inputs are finite; a program needn't handle non-finite values.
Results may differ from a plain program's by a relative error of at most 0.0001.
Values sent between devices are 32-bit elements; how exact they have to be, the bound alone decides.
A program may use at most 128 MiB of HBM per device.

v0:
```python
import jax
import jax.numpy as jnp
from jax import lax
from jax.experimental import pallas as pl
from jax.experimental.pallas import tpu as pltpu
from jax.sharding import PartitionSpec as P

RMAX = 6
TMAX = 6
MESH = pl.DeviceIdType.MESH

V_COPIES = ((1, 0, 2), (0, 1, 2), (1, 1, 2), (0, 2, 1), (1, 2, 1))
E_COPIES = (
    (1, 0, 1, 3),
    (2, 0, 0, 3),
    (0, 1, 2, 3),
    (1, 1, 1, 3),
    (2, 1, 0, 3),
    (1, 2, 1, 2),
    (2, 2, 0, 2),
)
PARTNERS = tuple((a, g) for a in range(3) for g in range(3) if a or g)


def cmul(a, b):
    return a[0] * b[0] - a[1] * b[1], a[0] * b[1] + a[1] * b[0]


def cmul_conj(a, b):
    return a[0] * b[0] + a[1] * b[1], a[1] * b[0] - a[0] * b[1]


def csum(terms):
    real, imag = terms[0]
    for term in terms[1:]:
        real, imag = real + term[0], imag + term[1]
    return real, imag


def matmul(a, b):
    return [[csum([cmul(row[j], b[j][k]) for j in range(3)]) for k in range(3)] for row in a]


def matmul_dagger(a, b):
    return [[csum([cmul_conj(row[j], b[k][j]) for j in range(3)]) for k in range(3)] for row in a]


def third_row(a):
    row = []
    for i in range(3):
        j, k = (i + 1) % 3, (i + 2) % 3
        first = cmul(a[0][j], a[1][k])
        second = cmul(a[0][k], a[1][j])
        row.append((first[0] - second[0], second[1] - first[1]))
    return [a[0], a[1], row]


def per_element(function, *matrices):
    return [
        [tuple(function(*(m[i][j][c] for m in matrices)) for c in range(2)) for j in range(3)]
        for i in range(len(matrices[0]))
    ]


def load(ref, lead, rows, window=slice(None)):
    return [
        [tuple(ref[(*lead, c * 3 * rows + i * 3 + j, window)] for c in range(2)) for j in range(3)]
        for i in range(rows)
    ]


def store(ref, lead, matrix, rows, window=slice(None)):
    for c in range(2):
        for i in range(rows):
            for j in range(3):
                ref[(*lead, c * 3 * rows + i * 3 + j, window)] = matrix[i][j][c]


def roll(value, shift):
    shift = shift % 8
    return value if shift == 0 else pltpu.roll(value, shift, 0)


def kernel(
    sizes, link_x, link_t, out, ux, ut, field, edge, left, right, tiles, chain, tmp, part, peer,
    in_sem, v_send, v_recv, e_send, e_recv, sum_send, sum_recv,
):
    n_x, n_y, n_t = sizes
    x_at, y_at, t_at = lax.axis_index("gx"), lax.axis_index("gy"), lax.axis_index("ta")
    other_y = lax.rem(y_at + 1, n_y)

    barrier = pltpu.get_barrier_semaphore()
    for a, g in PARTNERS:
        above = {"gx": lax.rem(x_at + g, n_x), "ta": lax.rem(t_at + a, n_t)}
        pl.semaphore_signal(barrier, inc=1, device_id=above, device_id_type=MESH)
    pl.semaphore_signal(barrier, inc=1, device_id={"gy": other_y}, device_id_type=MESH)

    copy_x = pltpu.make_async_copy(link_x, ux, in_sem.at[0])
    copy_t = pltpu.make_async_copy(link_t, ut, in_sem.at[1])
    copy_x.start()
    copy_t.start()

    row = lax.broadcasted_iota(jnp.int32, (8, 128), 0)
    time = lax.rem(row, 4)
    lower = row < 4
    one = jnp.ones((8, 128), jnp.float32)
    zero = jnp.zeros((8, 128), jnp.float32)
    unit = [[(one if i == k else zero, zero) for k in range(3)] for i in range(3)]

    def pick(mask, a, b):
        return per_element(lambda p, q: jnp.where(mask, p, q), a, b)

    def rolled(a, shift):
        return per_element(lambda p: roll(p, shift), a)

    copy_x.wait()
    u0 = load(ux, (), 3, pl.ds(0, 8))
    u1 = load(ux, (), 3, pl.ds(8, 8))
    halves = matmul(pick(lower, u0, rolled(u1, 4)), pick(lower, rolled(u0, 4), u1))
    whole = matmul(pick(lower, halves, rolled(halves, 4)), pick(lower, u1, halves))
    starts = [
        pick(lower, unit, rolled(u0, 4)),
        pick(lower, halves, rolled(whole, 4)),
    ]
    store(edge, (0, 0, 2), per_element(lambda p: p[4:8], whole[:2]), 2)
    copy_t.wait()
    links = []
    for xp in range(2):
        begin = starts[xp]
        end = pick(time == 3, unit, rolled(begin, 7))
        v = matmul_dagger(matmul(begin[:2], load(ut, (), 3, pl.ds(8 * xp, 8))), end)
        store(field, (0, xp), v, 2)
        links.append(v)

    def first_times(low, high):
        value = jnp.where(row == 0, low, roll(low, -3))
        value = jnp.where(row == 2, roll(high, 2), value)
        return jnp.where(row == 3, roll(high, -1), value)[0:4]

    store(edge, (0, 0, 0), per_element(first_times, links[0], links[1]), 2)
    store(edge, (0, 0, 1), per_element(first_times, starts[0][:2], starts[1][:2]), 2)

    pl.semaphore_wait(barrier, len(PARTNERS) + 1)

    v_copies, e_copies = {}, {}
    order = [("e", i) for i in range(len(E_COPIES))] + [("v", i) for i in range(len(V_COPIES))]
    for kind, i in order:
        a, g = (V_COPIES if kind == "v" else E_COPIES)[i][:2]
        below = {"gx": lax.rem(x_at + n_x - g, n_x), "ta": lax.rem(t_at + n_t - a, n_t)}
        if kind == "v":
            pairs = V_COPIES[i][2]
            copy = pltpu.make_async_remote_copy(
                src_ref=field.at[0, pl.ds(0, pairs)],
                dst_ref=field.at[a, pl.ds(2 * g, pairs)],
                send_sem=v_send.at[i],
                recv_sem=v_recv.at[i],
                device_id=below,
                device_id_type=MESH,
            )
            v_copies[a, g] = copy
        else:
            first, last = E_COPIES[i][2:]
            copy = pltpu.make_async_remote_copy(
                src_ref=edge.at[0, 0, pl.ds(first, last - first)],
                dst_ref=edge.at[a, g, pl.ds(first, last - first)],
                send_sem=e_send.at[i],
                recv_sem=e_recv.at[i],
                device_id=below,
                device_id_type=MESH,
            )
            e_copies[a, g] = copy
        copy.start()

    def arrived(g):
        for copies in (e_copies, v_copies):
            for a in range(3):
                if (a, g) in copies:
                    copies[a, g].wait_recv()

    def both_halves(a, g):
        value = load(edge, (a, g, 2), 2)
        store(tmp, (), value, 2, pl.ds(0, 4))
        store(tmp, (), value, 2, pl.ds(4, 4))
        return third_row(load(tmp, (), 2))

    def spread(matrix, rows, first):
        return per_element(lambda p: jnp.broadcast_to(p[first : first + 1], (8, 128)), matrix[:rows])

    def change_of_gauge(g):
        previous = None
        for a in (2, 1, 0):
            value = both_halves(a, 0)
            if g == 2:
                if a == 2:
                    value = matmul(value, both_halves(2, 1))
                else:
                    value = matmul(value, both_halves(a, 1))
            if a == 2:
                store(left, (2,), spread(value, 2, 0), 2)
                store(right, (2,), spread(value, 3, 1), 3)
            else:
                store(left, (a,), value[:2], 2)
                after = pick(time == 3, previous, rolled(value, 7))
                store(right, (a,), after, 3)
            previous = spread(value, 3, 0)

    def row_pair(a, g, piece, q):
        low = load(edge, (a, g, piece), 2, pl.ds(2 * q, 1))
        high = load(edge, (a, g, piece), 2, pl.ds(2 * q + 1, 1))
        wide = lambda p: jnp.broadcast_to(p, (8, 128))
        return third_row(per_element(lambda p, s: jnp.where(lower, wide(p), wide(s)), low, high))

    def into_window(value, a, g):
        if g > 0:
            value = third_row(matmul_dagger(value, load(right, (a,), 3)))
            value = matmul(load(left, (a,), 2), value)
        return third_row(value)

    def pair(g, q):
        xp = 2 * g + q
        for a in range(2):
            fix = pick(time == 3, row_pair(a + 1, g, 1, q), unit)
            value = matmul_dagger(load(field, (a, xp), 2), fix)
            store(tiles, (a,), into_window(value, a, g), 3)
        store(tiles, (2,), into_window(row_pair(2, g, 0, q)[:2], 2, g), 3)
        product = load(tiles, (0,), 3)
        store(chain, (0, xp), product, 3)
        for k in range(1, TMAX):
            if k < 4:
                here, after = load(tiles, (0,), 3), load(tiles, (1,), 3)
                factor = pick(time < 4 - k, rolled(here, -k), rolled(after, 4 - k))
            elif k == 4:
                factor = load(tiles, (1,), 3)
            else:
                factor = pick(time < 3, rolled(load(tiles, (1,), 3), -1), load(tiles, (2,), 3))
            product = third_row(matmul(product[:2], factor))
            store(chain, (k, xp), product, 3)

    for g in range(3):
        arrived(g)
        if g > 0:
            change_of_gauge(g)

        def body(q, carry, g=g):
            pair(g, q)
            return carry

        lax.fori_loop(0, 2 if g < 2 else 1, body, 0)

    lane = lax.broadcasted_iota(jnp.int32, (8, 128), 1)

    def correlate(u, sums):
        totals = [None] * (2 * RMAX)
        for c in range(18):
            even = [chain[u, m, c] for m in range(5)]
            turned = [roll(value, 4) for value in even]
            odd = [jnp.where(lower, turned[m], turned[m + 1]) for m in range(4)]
            for r in range(1, RMAX + 1):
                for xp in range(2):
                    far = odd[xp + r // 2] if r % 2 else even[xp + r // 2]
                    i = 2 * (r - 1) + xp
                    term = even[xp] * far
                    totals[i] = term if totals[i] is None else totals[i] + term
        for i in range(2 * RMAX):
            total = jnp.sum(totals[i], axis=1, keepdims=True)
            sums = jnp.where(lane == u * (2 * RMAX) + i, total, sums)
        return sums

    part[...] = lax.fori_loop(0, TMAX, correlate, zero)

    for copies in (e_copies, v_copies):
        for copy in copies.values():
            copy.wait_send()
    swap = pltpu.make_async_remote_copy(
        src_ref=part,
        dst_ref=peer,
        send_sem=sum_send,
        recv_sem=sum_recv,
        device_id={"gy": other_y},
        device_id_type=MESH,
    )
    swap.start()
    swap.wait()
    out[...] = (part[...] + peer[...]) / (3.0 * 128 * n_y)


def solution(mesh):
    sizes = tuple(mesh.shape[name] for name in ("gx", "gy", "ta"))

    def local(link_x, link_t):
        vmem = lambda *shape: pltpu.VMEM(shape, jnp.float32)
        sums = pl.pallas_call(
            lambda *refs: kernel(sizes, *refs),
            out_shape=jax.ShapeDtypeStruct((8, 128), jnp.float32),
            in_specs=[pl.BlockSpec(memory_space=pl.ANY)] * 2,
            out_specs=pl.BlockSpec(memory_space=pltpu.VMEM),
            scratch_shapes=[
                vmem(18, 16, 128),
                vmem(18, 16, 128),
                vmem(2, 5, 12, 8, 128),
                vmem(3, 3, 3, 12, 4, 128),
                vmem(3, 12, 8, 128),
                vmem(3, 18, 8, 128),
                vmem(3, 18, 8, 128),
                vmem(TMAX, 5, 18, 8, 128),
                vmem(12, 8, 128),
                vmem(8, 128),
                vmem(8, 128),
                pltpu.SemaphoreType.DMA((2,)),
                pltpu.SemaphoreType.DMA((len(V_COPIES),)),
                pltpu.SemaphoreType.DMA((len(V_COPIES),)),
                pltpu.SemaphoreType.DMA((len(E_COPIES),)),
                pltpu.SemaphoreType.DMA((len(E_COPIES),)),
                pltpu.SemaphoreType.DMA,
                pltpu.SemaphoreType.DMA,
            ],
            compiler_params=pltpu.CompilerParams(collective_id=0, has_side_effects=True),
        )(link_x.reshape(18, 16, 128), link_t.reshape(18, 16, 128))
        sums = sums[:, : 12 * TMAX].reshape(2, 4, TMAX, RMAX, 2)
        return sums.transpose(3, 2, 4, 0, 1).reshape(RMAX, TMAX, 4, 4)

    return jax.shard_map(
        local,
        mesh=mesh,
        in_specs=(P(None, None, None, "gx", "ta", "gy"),) * 2,
        out_specs=P(None, None, "gx", "ta"),
        check_vma=False,
    )
```

profile of v0, /device:TPU:1, one launch (start us, length us, event | category | flops | bytes accessed | tf_op | source)
XLA Modules:
  0.0 27.3 jit_solution(5088040868204364445)
XLA Ops:
  0.0 25.5 %shard_map.28 = f32[8,128]{1,0:T(8,128)} custom-call(f32[18,16,128]{2,1,0:T(8,128)} %bitcast.9, f32[18,16,128]{2,1,0:T(8,128)} %bitcast.10), custom_call_target="tpu_custom_call" | custom-call | tf_op jit(solution)/shard_map/pallas_call | solution.py:292
  25.6 0.8 %copy.4 = f32[8,72]{0,1:T(8,128)S(1)} copy(f32[8,72]{1,0:T(8,128)} %bitcast.11) | data formatting | bytes 4608 | tf_op jit(solution)/shard_map/slice | solution.py:319
  26.3 0.1 reshape.14
  26.4 0.9 %copy.5 = f32[6,6,4,4]{1,3,2,0:T(4,128)} copy(f32[6,6,4,4]{3,2,0,1:T(4,128)S(1)} %bitcast.8) | data formatting | bytes 4608 | tf_op jit(solution)/shard_map/reshape | solution.py:320
where the time goes:
time: 27.4 us; the launch traced here: 27.3 us
  Pallas kernels  25.5 us (93%)
  local copies, waits for them, and re-layouts  1.74 us (6%)
    pallas_call x1, Pallas kernels, local(): pl.pallas_call(lambda *refs: kernel(sizes, *refs), out_shape=jax.ShapeDty...  25.5 us
    reshape x1, local copies, waits for them, and re-layouts, local(): return sums.transpose(3, 2, 4, 0, 1).reshape(RMAX, TMAX, 4, 4)  0.87 us
    slice x1, local copies, waits for them, and re-layouts, local(): sums = sums[:, :12 * TMAX].reshape(2, 4, TMAX, RMAX, 2)  0.77 us

commit v1 on v0

--- a/solution.py
+++ b/solution.py
@@ -83,16 +83,29 @@
 
 def kernel(
     sizes, link_x, link_t, out, ux, ut, field, edge, left, right, tiles, chain, tmp, part, peer,
-    in_sem, v_send, v_recv, e_send, e_recv, sum_send, sum_recv,
+    in_sem, ready, v_send, v_recv, e_send, e_recv, sum_send, sum_recv,
 ):
     n_x, n_y, n_t = sizes
     x_at, y_at, t_at = lax.axis_index("gx"), lax.axis_index("gy"), lax.axis_index("ta")
     other_y = lax.rem(y_at + 1, n_y)
 
+    def above(a, g):
+        return {"gx": lax.rem(x_at + g, n_x), "ta": lax.rem(t_at + a, n_t)}
+
+    def below(a, g):
+        return {"gx": lax.rem(x_at + n_x - g, n_x), "ta": lax.rem(t_at + n_t - a, n_t)}
+
     barrier = pltpu.get_barrier_semaphore()
     for a, g in PARTNERS:
-        above = {"gx": lax.rem(x_at + g, n_x), "ta": lax.rem(t_at + a, n_t)}
-        pl.semaphore_signal(barrier, inc=1, device_id=above, device_id_type=MESH)
+
+        @pl.when(t_at + a < n_t)
+        def _():
+            pl.semaphore_signal(barrier, inc=1, device_id=above(a, g), device_id_type=MESH)
+
+        @pl.when(t_at < a)
+        def _():
+            pl.semaphore_signal(barrier, inc=1, device_id=below(a, g), device_id_type=MESH)
+
     pl.semaphore_signal(barrier, inc=1, device_id={"gy": other_y}, device_id_type=MESH)
 
     copy_x = pltpu.make_async_copy(link_x, ux, in_sem.at[0])
@@ -140,13 +153,23 @@
     store(edge, (0, 0, 0), per_element(first_times, links[0], links[1]), 2)
     store(edge, (0, 0, 1), per_element(first_times, starts[0][:2], starts[1][:2]), 2)
 
-    pl.semaphore_wait(barrier, len(PARTNERS) + 1)
+    peers = 1
+    for a, _ in PARTNERS:
+        peers += (t_at >= a).astype(jnp.int32) if a else 1
+        peers += (t_at + a >= n_t).astype(jnp.int32) if a else 0
+    pl.semaphore_wait(barrier, peers)
+
+    for k, (a, g) in enumerate(PARTNERS):
+
+        @pl.when(t_at + a >= n_t)
+        def _():
+            pl.semaphore_signal(ready.at[k], inc=1, device_id=above(a, g), device_id_type=MESH)
+
 
     v_copies, e_copies = {}, {}
     order = [("e", i) for i in range(len(E_COPIES))] + [("v", i) for i in range(len(V_COPIES))]
     for kind, i in order:
         a, g = (V_COPIES if kind == "v" else E_COPIES)[i][:2]
-        below = {"gx": lax.rem(x_at + n_x - g, n_x), "ta": lax.rem(t_at + n_t - a, n_t)}
         if kind == "v":
             pairs = V_COPIES[i][2]
             copy = pltpu.make_async_remote_copy(
@@ -154,7 +177,7 @@
                 dst_ref=field.at[a, pl.ds(2 * g, pairs)],
                 send_sem=v_send.at[i],
                 recv_sem=v_recv.at[i],
-                device_id=below,
+                device_id=below(a, g),
                 device_id_type=MESH,
             )
             v_copies[a, g] = copy
@@ -165,11 +188,23 @@
                 dst_ref=edge.at[a, g, pl.ds(first, last - first)],
                 send_sem=e_send.at[i],
                 recv_sem=e_recv.at[i],
-                device_id=below,
+                device_id=below(a, g),
                 device_id_type=MESH,
             )
             e_copies[a, g] = copy
-        copy.start()
+        if a:
+            pl.when(t_at >= a)(copy.start)
+        else:
+            copy.start()
+
+    for k, (a, g) in enumerate(PARTNERS):
+
+        @pl.when(t_at < a)
+        def _():
+            pl.semaphore_wait(ready.at[k], 1)
+            for copies in (e_copies, v_copies):
+                if (a, g) in copies:
+                    copies[a, g].start()
 
     def arrived(g):
         for copies in (e_copies, v_copies):
@@ -236,37 +271,59 @@
             product = third_row(matmul(product[:2], factor))
             store(chain, (k, xp), product, 3)
 
-    for g in range(3):
-        arrived(g)
-        if g > 0:
-            change_of_gauge(g)
-
-        def body(q, carry, g=g):
+    lane = lax.broadcasted_iota(jnp.int32, (8, 128), 1)
+
+    def correlate(sums, picked):
+        def body(u, sums):
+            totals = {}
+            for c in range(18):
+                tile = {}
+
+                def even(m):
+                    if m not in tile:
+                        tile[m] = chain[u, m, c]
+                    return tile[m]
+
+                def turned(m):
+                    if ("t", m) not in tile:
+                        tile["t", m] = roll(even(m), 4)
+                    return tile["t", m]
+
+                def odd(m):
+                    if ("o", m) not in tile:
+                        tile["o", m] = jnp.where(lower, turned(m), turned(m + 1))
+                    return tile["o", m]
+
+                for r, xp in picked:
+                    far = odd(xp + r // 2) if r % 2 else even(xp + r // 2)
+                    term = even(xp) * far
+                    totals[r, xp] = totals[r, xp] + term if (r, xp) in totals else term
+            for r, xp in picked:
+                total = jnp.sum(totals[r, xp], axis=1, keepdims=True)
+                sums = jnp.where(lane == 8 * (2 * (r - 1) + xp) + u, total, sums)
+            return sums
+
+        return lax.fori_loop(0, TMAX, body, sums)
+
+    def chains(g):
+        def body(q, carry):
             pair(g, q)
             return carry
 
         lax.fori_loop(0, 2 if g < 2 else 1, body, 0)
 
-    lane = lax.broadcasted_iota(jnp.int32, (8, 128), 1)
-
-    def correlate(u, sums):
-        totals = [None] * (2 * RMAX)
-        for c in range(18):
-            even = [chain[u, m, c] for m in range(5)]
-            turned = [roll(value, 4) for value in even]
-            odd = [jnp.where(lower, turned[m], turned[m + 1]) for m in range(4)]
-            for r in range(1, RMAX + 1):
-                for xp in range(2):
-                    far = odd[xp + r // 2] if r % 2 else even[xp + r // 2]
-                    i = 2 * (r - 1) + xp
-                    term = even[xp] * far
-                    totals[i] = term if totals[i] is None else totals[i] + term
-        for i in range(2 * RMAX):
-            total = jnp.sum(totals[i], axis=1, keepdims=True)
-            sums = jnp.where(lane == u * (2 * RMAX) + i, total, sums)
-        return sums
-
-    part[...] = lax.fori_loop(0, TMAX, correlate, zero)
+    loops = [(r, xp) for r in range(1, RMAX + 1) for xp in range(2)]
+    last = [(r, xp) for r, xp in loops if xp + (r + 1) // 2 == 4]
+    arrived(0)
+    change_of_gauge(1)
+    chains(0)
+    arrived(1)
+    chains(1)
+    change_of_gauge(2)
+    sums = correlate(zero, [loop for loop in loops if loop not in last])
+    arrived(2)
+    chains(2)
+    part[...] = correlate(sums, last)
 
     for copies in (e_copies, v_copies):
         for copy in copies.values():
@@ -281,7 +338,12 @@
     )
     swap.start()
     swap.wait()
-    out[...] = (part[...] + peer[...]) / (3.0 * 128 * n_y)
+    sums = (part[...] + peer[...]) / (3.0 * 128 * n_y)
+    for r, xp in loops:
+        at = 8 * (2 * (r - 1) + xp)
+        value = sums if at == 0 else pltpu.roll(sums, 128 - at, 1)
+        out[r - 1, 2 * xp] = value[0:4, 0:TMAX]
+        out[r - 1, 2 * xp + 1] = value[4:8, 0:TMAX]
 
 
 def solution(mesh):
@@ -291,7 +353,7 @@
         vmem = lambda *shape: pltpu.VMEM(shape, jnp.float32)
         sums = pl.pallas_call(
             lambda *refs: kernel(sizes, *refs),
-            out_shape=jax.ShapeDtypeStruct((8, 128), jnp.float32),
+            out_shape=jax.ShapeDtypeStruct((RMAX, 4, 4, TMAX), jnp.float32),
             in_specs=[pl.BlockSpec(memory_space=pl.ANY)] * 2,
             out_specs=pl.BlockSpec(memory_space=pltpu.VMEM),
             scratch_shapes=[
@@ -307,6 +369,7 @@
                 vmem(8, 128),
                 vmem(8, 128),
                 pltpu.SemaphoreType.DMA((2,)),
+                pltpu.SemaphoreType.REGULAR((len(PARTNERS),)),
                 pltpu.SemaphoreType.DMA((len(V_COPIES),)),
                 pltpu.SemaphoreType.DMA((len(V_COPIES),)),
                 pltpu.SemaphoreType.DMA((len(E_COPIES),)),
@@ -316,8 +379,7 @@
             ],
             compiler_params=pltpu.CompilerParams(collective_id=0, has_side_effects=True),
         )(link_x.reshape(18, 16, 128), link_t.reshape(18, 16, 128))
-        sums = sums[:, : 12 * TMAX].reshape(2, 4, TMAX, RMAX, 2)
-        return sums.transpose(3, 2, 4, 0, 1).reshape(RMAX, TMAX, 4, 4)
+        return sums.transpose(0, 3, 1, 2)
 
     return jax.shard_map(
         local,

time: 27.4 us -> 28.8 us (1.051)
  the two profiles are of different devices: /device:TPU:1 before, /device:TPU:224 now
where the time goes in v1:
time: 28.8 us; the launch traced here: 28.6 us
  Pallas kernels  27.2 us (94%)
  local copies, waits for them, and re-layouts  1.42 us (5%)
    pallas_call x1, Pallas kernels, local(): pl.pallas_call(lambda *refs: kernel(sizes, *refs), out_shape=jax.ShapeDty...  27.2 us
    unnamed x1, local copies, waits for them, and re-layouts  1.42 us

profile of v1, /device:TPU:224, one launch (start us, length us, event | category | flops | bytes accessed | tf_op | source)
XLA Modules:
  0.0 28.6 jit_solution(3499388693486921232)
XLA Ops:
  0.0 27.2 %shard_map.28 = f32[6,4,4,6]{3,2,1,0:T(4,128)} custom-call(f32[18,16,128]{2,1,0:T(8,128)} %bitcast.4, f32[18,16,128]{2,1,0:T(8,128)} %bitcast.5), custom_call_target="tpu_custom_call" | custom-call | tf_op jit(solution)/shard_map/pallas_call | solution.py:354
  27.2 1.4 %copy.4 = f32[6,6,4,4]{1,3,2,0:T(4,128)} copy(f32[6,6,4,4]{1,3,2,0:T(4,128)} %bitcast.3) | data formatting | bytes 4608

commit v2 on v1

--- a/solution.py
+++ b/solution.py
@@ -83,7 +83,7 @@
 
 def kernel(
     sizes, link_x, link_t, out, ux, ut, field, edge, left, right, tiles, chain, tmp, part, peer,
-    in_sem, ready, v_send, v_recv, e_send, e_recv, sum_send, sum_recv,
+    in_sem, ready, y_ready, v_send, v_recv, v_pass, e_send, e_recv, e_pass, sum_send, sum_recv,
 ):
     n_x, n_y, n_t = sizes
     x_at, y_at, t_at = lax.axis_index("gx"), lax.axis_index("gy"), lax.axis_index("ta")
@@ -96,17 +96,54 @@
         return {"gx": lax.rem(x_at + n_x - g, n_x), "ta": lax.rem(t_at + n_t - a, n_t)}
 
     barrier = pltpu.get_barrier_semaphore()
+    def always(*conditions):
+        known = [c for c in conditions if isinstance(c, bool)]
+        traced = [c for c in conditions if not isinstance(c, bool)]
+        if not all(known):
+            return False
+        result = True
+        for c in traced:
+            result = c if result is True else result & c
+        return result
+
+    def when(condition, action):
+        if condition is True:
+            action()
+        elif condition is not False:
+            pl.when(condition)(action)
+
+    odd = lax.rem(x_at, 2) == 1
+    even = lax.rem(x_at, 2) == 0
+
+    def sends(a, g):
+        return odd if g == 2 else even if g == 1 and a > 0 else True
+
+    def receives(a, g):
+        return odd if g == 2 or (g == 1 and a > 0) else True
+
+    def sends_over_end(a, g):
+        return (t_at < a) | (x_at < g)
+
+    def receives_over_end(a, g):
+        return (t_at + a >= n_t) | (x_at + g >= n_x)
+
+    peers = (y_at > 0).astype(jnp.int32)
     for a, g in PARTNERS:
 
-        @pl.when(t_at + a < n_t)
+        @pl.when(always(receives(a, g), jnp.logical_not(receives_over_end(a, g))))
         def _():
             pl.semaphore_signal(barrier, inc=1, device_id=above(a, g), device_id_type=MESH)
 
-        @pl.when(t_at < a)
+        @pl.when(always(sends(a, g), sends_over_end(a, g)))
         def _():
             pl.semaphore_signal(barrier, inc=1, device_id=below(a, g), device_id_type=MESH)
 
-    pl.semaphore_signal(barrier, inc=1, device_id={"gy": other_y}, device_id_type=MESH)
+        peers += always(sends(a, g), jnp.logical_not(sends_over_end(a, g))).astype(jnp.int32)
+        peers += always(receives(a, g), receives_over_end(a, g)).astype(jnp.int32)
+
+    @pl.when(y_at == 0)
+    def _():
+        pl.semaphore_signal(barrier, inc=1, device_id={"gy": other_y}, device_id_type=MESH)
 
     copy_x = pltpu.make_async_copy(link_x, ux, in_sem.at[0])
     copy_t = pltpu.make_async_copy(link_t, ut, in_sem.at[1])
@@ -153,64 +190,84 @@
     store(edge, (0, 0, 0), per_element(first_times, links[0], links[1]), 2)
     store(edge, (0, 0, 1), per_element(first_times, starts[0][:2], starts[1][:2]), 2)
 
-    peers = 1
-    for a, _ in PARTNERS:
-        peers += (t_at >= a).astype(jnp.int32) if a else 1
-        peers += (t_at + a >= n_t).astype(jnp.int32) if a else 0
-    pl.semaphore_wait(barrier, peers)
+
+    @pl.when(peers > 0)
+    def _():
+        pl.semaphore_wait(barrier, peers)
 
     for k, (a, g) in enumerate(PARTNERS):
 
-        @pl.when(t_at + a >= n_t)
+        @pl.when(always(receives(a, g), receives_over_end(a, g)))
         def _():
             pl.semaphore_signal(ready.at[k], inc=1, device_id=above(a, g), device_id_type=MESH)
 
-
-    v_copies, e_copies = {}, {}
-    order = [("e", i) for i in range(len(E_COPIES))] + [("v", i) for i in range(len(V_COPIES))]
-    for kind, i in order:
-        a, g = (V_COPIES if kind == "v" else E_COPIES)[i][:2]
-        if kind == "v":
-            pairs = V_COPIES[i][2]
-            copy = pltpu.make_async_remote_copy(
-                src_ref=field.at[0, pl.ds(0, pairs)],
-                dst_ref=field.at[a, pl.ds(2 * g, pairs)],
-                send_sem=v_send.at[i],
-                recv_sem=v_recv.at[i],
-                device_id=below(a, g),
-                device_id_type=MESH,
-            )
-            v_copies[a, g] = copy
-        else:
-            first, last = E_COPIES[i][2:]
-            copy = pltpu.make_async_remote_copy(
-                src_ref=edge.at[0, 0, pl.ds(first, last - first)],
-                dst_ref=edge.at[a, g, pl.ds(first, last - first)],
-                send_sem=e_send.at[i],
-                recv_sem=e_recv.at[i],
-                device_id=below(a, g),
-                device_id_type=MESH,
-            )
-            e_copies[a, g] = copy
-        if a:
-            pl.when(t_at >= a)(copy.start)
-        else:
+    @pl.when(y_at > 0)
+    def _():
+        pl.semaphore_signal(y_ready, inc=1, device_id={"gy": other_y}, device_id_type=MESH)
+
+    def v_copy(i, a, g, target, send_sem):
+        to_a, to_g, pairs = V_COPIES[i]
+        return pltpu.make_async_remote_copy(
+            src_ref=field.at[a, pl.ds(2 * g, pairs)],
+            dst_ref=field.at[to_a, pl.ds(2 * to_g, pairs)],
+            send_sem=send_sem.at[i],
+            recv_sem=v_recv.at[i],
+            device_id=target,
+            device_id_type=MESH,
+        )
+
+    def e_copy(i, a, g, target, send_sem):
+        to_a, to_g, first, last = E_COPIES[i]
+        return pltpu.make_async_remote_copy(
+            src_ref=edge.at[a, g, pl.ds(first, last - first)],
+            dst_ref=edge.at[to_a, to_g, pl.ds(first, last - first)],
+            send_sem=send_sem.at[i],
+            recv_sem=e_recv.at[i],
+            device_id=target,
+            device_id_type=MESH,
+        )
+
+    copies = {partner: [] for partner in PARTNERS}
+    passed_on = {partner: [] for partner in PARTNERS}
+    for make, table, own_sem, pass_sem in (
+        (e_copy, E_COPIES, e_send, e_pass),
+        (v_copy, V_COPIES, v_send, v_pass),
+    ):
+        for i, entry in enumerate(table):
+            a, g = entry[:2]
+            copies[a, g].append(make(i, 0, 0, below(a, g), own_sem))
+            if g == 2 or (g == 1 and a > 0):
+                passed_on[a, g].append(make(i, a, g - 1, below(0, 1), pass_sem))
+
+    def start(partner):
+        for copy in copies[partner]:
             copy.start()
 
-    for k, (a, g) in enumerate(PARTNERS):
-
-        @pl.when(t_at < a)
+    by_block = sorted(PARTNERS, key=lambda partner: partner[1])
+    for a, g in by_block:
+        when(
+            always(sends(a, g), jnp.logical_not(sends_over_end(a, g))),
+            lambda a=a, g=g: start((a, g)),
+        )
+    for a, g in by_block:
+
+        @pl.when(always(sends(a, g), sends_over_end(a, g)))
         def _():
-            pl.semaphore_wait(ready.at[k], 1)
-            for copies in (e_copies, v_copies):
-                if (a, g) in copies:
-                    copies[a, g].start()
+            pl.semaphore_wait(ready.at[PARTNERS.index((a, g))], 1)
+            start((a, g))
 
     def arrived(g):
-        for copies in (e_copies, v_copies):
-            for a in range(3):
-                if (a, g) in copies:
-                    copies[a, g].wait_recv()
+        for a in range(3):
+            if a or g:
+                for copy in copies[a, g]:
+                    copy.wait_recv()
+        if g < 2:
+
+            @pl.when(odd)
+            def _():
+                for a in range(3):
+                    for copy in passed_on.get((a, g + 1), ()):
+                        copy.start()
 
     def both_halves(a, g):
         value = load(edge, (a, g, 2), 2)
@@ -325,9 +382,20 @@
     chains(2)
     part[...] = correlate(sums, last)
 
-    for copies in (e_copies, v_copies):
-        for copy in copies.values():
-            copy.wait_send()
+    for a, g in PARTNERS:
+
+        def sent(a=a, g=g):
+            for copy in copies[a, g]:
+                copy.wait_send()
+
+        when(sends(a, g), sent)
+
+    @pl.when(odd)
+    def _():
+        for partner in PARTNERS:
+            for copy in passed_on[partner]:
+                copy.wait_send()
+
     swap = pltpu.make_async_remote_copy(
         src_ref=part,
         dst_ref=peer,
@@ -336,6 +404,11 @@
         device_id={"gy": other_y},
         device_id_type=MESH,
     )
+
+    @pl.when(y_at == 0)
+    def _():
+        pl.semaphore_wait(y_ready, 1)
+
     swap.start()
     swap.wait()
     sums = (part[...] + peer[...]) / (3.0 * 128 * n_y)
@@ -370,8 +443,11 @@
                 vmem(8, 128),
                 pltpu.SemaphoreType.DMA((2,)),
                 pltpu.SemaphoreType.REGULAR((len(PARTNERS),)),
+                pltpu.SemaphoreType.REGULAR,
                 pltpu.SemaphoreType.DMA((len(V_COPIES),)),
                 pltpu.SemaphoreType.DMA((len(V_COPIES),)),
+                pltpu.SemaphoreType.DMA((len(V_COPIES),)),
+                pltpu.SemaphoreType.DMA((len(E_COPIES),)),
                 pltpu.SemaphoreType.DMA((len(E_COPIES),)),
                 pltpu.SemaphoreType.DMA((len(E_COPIES),)),
                 pltpu.SemaphoreType.DMA,

time: 28.8 us -> 24.1 us (0.84)
  the two profiles are of different devices: /device:TPU:224 before, /device:TPU:225 now
where the time goes in v2:
time: 24.1 us; the launch traced here: 24 us
  Pallas kernels  22.6 us (94%)
  local copies, waits for them, and re-layouts  1.42 us (6%)
    pallas_call x1, Pallas kernels, local(): pl.pallas_call(lambda *refs: kernel(sizes, *refs), out_shape=jax.ShapeDty...  22.6 us
    unnamed x1, local copies, waits for them, and re-layouts  1.42 us

profile of v2, /device:TPU:225, one launch (start us, length us, event | category | flops | bytes accessed | tf_op | source)
XLA Modules:
  0.0 24.0 jit_solution(15384706844079706896)
XLA Ops:
  0.0 22.6 %shard_map.28 = f32[6,4,4,6]{3,2,1,0:T(4,128)} custom-call(f32[18,16,128]{2,1,0:T(8,128)} %bitcast.4, f32[18,16,128]{2,1,0:T(8,128)} %bitcast.5), custom_call_target="tpu_custom_call" | custom-call | tf_op jit(solution)/shard_map/pallas_call | solution.py:427
  22.6 1.4 %copy.4 = f32[6,6,4,4]{1,3,2,0:T(4,128)} copy(f32[6,6,4,4]{1,3,2,0:T(4,128)} %bitcast.3) | data formatting | bytes 4608

commit v3 on v2

--- a/solution.py
+++ b/solution.py
@@ -19,7 +19,7 @@
     (1, 2, 1, 2),
     (2, 2, 0, 2),
 )
-PARTNERS = tuple((a, g) for a in range(3) for g in range(3) if a or g)
+PARTNERS = ((1, 0), (2, 0), (0, 1), (0, 2))
 
 
 def cmul(a, b):
@@ -83,7 +83,8 @@
 
 def kernel(
     sizes, link_x, link_t, out, ux, ut, field, edge, left, right, tiles, chain, tmp, part, peer,
-    in_sem, ready, y_ready, v_send, v_recv, v_pass, e_send, e_recv, e_pass, sum_send, sum_recv,
+    in_sem, ready, y_ready, v_send, v_recv, v_next, v_second,
+    e_send, e_recv, e_next, e_second, sum_send, sum_recv,
 ):
     n_x, n_y, n_t = sizes
     x_at, y_at, t_at = lax.axis_index("gx"), lax.axis_index("gy"), lax.axis_index("ta")
@@ -113,13 +114,12 @@
             pl.when(condition)(action)
 
     odd = lax.rem(x_at, 2) == 1
-    even = lax.rem(x_at, 2) == 0
 
     def sends(a, g):
-        return odd if g == 2 else even if g == 1 and a > 0 else True
+        return odd if g == 2 else True
 
     def receives(a, g):
-        return odd if g == 2 or (g == 1 and a > 0) else True
+        return odd if g == 2 else True
 
     def sends_over_end(a, g):
         return (t_at < a) | (x_at < g)
@@ -227,47 +227,54 @@
             device_id_type=MESH,
         )
 
-    copies = {partner: [] for partner in PARTNERS}
-    passed_on = {partner: [] for partner in PARTNERS}
-    for make, table, own_sem, pass_sem in (
-        (e_copy, E_COPIES, e_send, e_pass),
-        (v_copy, V_COPIES, v_send, v_pass),
+    slots = [(a, g) for g in range(3) for a in range(3) if a or g]
+    copies = {slot: [] for slot in slots}
+    to_next = {slot: [] for slot in slots}
+    to_second = {slot: [] for slot in slots}
+    for make, table, own_sem, next_sem, second_sem in (
+        (e_copy, E_COPIES, e_send, e_next, e_second),
+        (v_copy, V_COPIES, v_send, v_next, v_second),
     ):
         for i, entry in enumerate(table):
             a, g = entry[:2]
             copies[a, g].append(make(i, 0, 0, below(a, g), own_sem))
             if g == 2 or (g == 1 and a > 0):
-                passed_on[a, g].append(make(i, a, g - 1, below(0, 1), pass_sem))
+                to_next[a, g - 1].append(make(i, a, g - 1, below(0, 1), next_sem))
+            if g == 2 and a > 0:
+                to_second[a, 0].append(make(i, a, 0, below(0, 2), second_sem))
 
     def start(partner):
         for copy in copies[partner]:
             copy.start()
 
-    by_block = sorted(PARTNERS, key=lambda partner: partner[1])
-    for a, g in by_block:
+    for a, g in PARTNERS:
         when(
             always(sends(a, g), jnp.logical_not(sends_over_end(a, g))),
             lambda a=a, g=g: start((a, g)),
         )
-    for a, g in by_block:
+    for a, g in PARTNERS:
 
         @pl.when(always(sends(a, g), sends_over_end(a, g)))
         def _():
             pl.semaphore_wait(ready.at[PARTNERS.index((a, g))], 1)
             start((a, g))
 
+    def each(some):
+        def start_all():
+            for copy in some:
+                copy.start()
+
+        return start_all
+
     def arrived(g):
-        for a in range(3):
-            if a or g:
+        for a, slot_g in slots:
+            if slot_g == g:
                 for copy in copies[a, g]:
                     copy.wait_recv()
-        if g < 2:
-
-            @pl.when(odd)
-            def _():
-                for a in range(3):
-                    for copy in passed_on.get((a, g + 1), ()):
-                        copy.start()
+                onward = to_next[a, g]
+                when(odd if g == 1 else bool(onward), each(onward))
+                if to_second[a, g]:
+                    when(odd, each(to_second[a, g]))
 
     def both_halves(a, g):
         value = load(edge, (a, g, 2), 2)
@@ -390,11 +397,19 @@
 
         when(sends(a, g), sent)
 
-    @pl.when(odd)
-    def _():
-        for partner in PARTNERS:
-            for copy in passed_on[partner]:
-                copy.wait_send()
+    for slot in slots:
+
+        def relayed(some):
+            def wait_all():
+                for copy in some:
+                    copy.wait_send()
+
+            return wait_all
+
+        if to_next[slot]:
+            when(odd if slot[1] == 1 else True, relayed(to_next[slot]))
+        if to_second[slot]:
+            when(odd, relayed(to_second[slot]))
 
     swap = pltpu.make_async_remote_copy(
         src_ref=part,
@@ -447,6 +462,8 @@
                 pltpu.SemaphoreType.DMA((len(V_COPIES),)),
                 pltpu.SemaphoreType.DMA((len(V_COPIES),)),
                 pltpu.SemaphoreType.DMA((len(V_COPIES),)),
+                pltpu.SemaphoreType.DMA((len(V_COPIES),)),
+                pltpu.SemaphoreType.DMA((len(E_COPIES),)),
                 pltpu.SemaphoreType.DMA((len(E_COPIES),)),
                 pltpu.SemaphoreType.DMA((len(E_COPIES),)),
                 pltpu.SemaphoreType.DMA((len(E_COPIES),)),

time: 24.1 us -> 23.5 us (0.975)
  the two profiles are of different devices: /device:TPU:225 before, /device:TPU:227 now
where the time goes in v3:
time: 23.5 us; the launch traced here: 23.4 us
  Pallas kernels  21.9 us (93%)
  local copies, waits for them, and re-layouts  1.42 us (6%)
    pallas_call x1, Pallas kernels, local(): pl.pallas_call(lambda *refs: kernel(sizes, *refs), out_shape=jax.ShapeDty...  21.9 us
    unnamed x1, local copies, waits for them, and re-layouts  1.42 us

profile of v3, /device:TPU:227, one launch (start us, length us, event | category | flops | bytes accessed | tf_op | source)
XLA Modules:
  0.0 23.4 jit_solution(15491923336412183086)
XLA Ops:
  0.0 21.9 %shard_map.28 = f32[6,4,4,6]{3,2,1,0:T(4,128)} custom-call(f32[18,16,128]{2,1,0:T(8,128)} %bitcast.4, f32[18,16,128]{2,1,0:T(8,128)} %bitcast.5), custom_call_target="tpu_custom_call" | custom-call | tf_op jit(solution)/shard_map/pallas_call | solution.py:442
  21.9 1.4 %copy.4 = f32[6,6,4,4]{1,3,2,0:T(4,128)} copy(f32[6,6,4,4]{1,3,2,0:T(4,128)} %bitcast.3) | data formatting | bytes 4608

commit v4 on v3

--- a/solution.py
+++ b/solution.py
@@ -9,7 +9,7 @@
 TMAX = 6
 MESH = pl.DeviceIdType.MESH
 
-V_COPIES = ((1, 0, 2), (0, 1, 2), (1, 1, 2), (0, 2, 1), (1, 2, 1))
+V_COPIES = ((1, 0, 0), (1, 0, 1), (0, 1, 0), (0, 1, 1), (1, 1, 0), (1, 1, 1), (0, 2, 0), (1, 2, 0))
 E_COPIES = (
     (1, 0, 1, 3),
     (2, 0, 0, 3),
@@ -19,7 +19,17 @@
     (1, 2, 1, 2),
     (2, 2, 0, 2),
 )
-PARTNERS = ((1, 0), (2, 0), (0, 1), (0, 2))
+PARTNERS = ((0, 1), (0, 2), (1, 0), (2, 0))
+ORDER = (
+    ("E", 1, 0),
+    ("E", 2, 0),
+    ("V", 0, 1, 0),
+    ("V", 1, 0, 0),
+    ("V", 0, 2, 0),
+    ("V", 1, 0, 1),
+    ("V", 0, 1, 1),
+    ("E", 0, 1),
+)
 
 
 def cmul(a, b):
@@ -206,10 +216,10 @@
         pl.semaphore_signal(y_ready, inc=1, device_id={"gy": other_y}, device_id_type=MESH)
 
     def v_copy(i, a, g, target, send_sem):
-        to_a, to_g, pairs = V_COPIES[i]
+        to_a, to_g, pair = V_COPIES[i]
         return pltpu.make_async_remote_copy(
-            src_ref=field.at[a, pl.ds(2 * g, pairs)],
-            dst_ref=field.at[to_a, pl.ds(2 * to_g, pairs)],
+            src_ref=field.at[a, 2 * g + pair],
+            dst_ref=field.at[to_a, 2 * to_g + pair],
             send_sem=send_sem.at[i],
             recv_sem=v_recv.at[i],
             device_id=target,
@@ -227,54 +237,44 @@
             device_id_type=MESH,
         )
 
-    slots = [(a, g) for g in range(3) for a in range(3) if a or g]
-    copies = {slot: [] for slot in slots}
-    to_next = {slot: [] for slot in slots}
-    to_second = {slot: [] for slot in slots}
-    for make, table, own_sem, next_sem, second_sem in (
-        (e_copy, E_COPIES, e_send, e_next, e_second),
-        (v_copy, V_COPIES, v_send, v_next, v_second),
+    copies, to_next, to_second = {}, {}, {}
+    for name, make, table, own_sem, next_sem, second_sem in (
+        ("E", e_copy, E_COPIES, e_send, e_next, e_second),
+        ("V", v_copy, V_COPIES, v_send, v_next, v_second),
     ):
         for i, entry in enumerate(table):
             a, g = entry[:2]
-            copies[a, g].append(make(i, 0, 0, below(a, g), own_sem))
+            tile = entry[2:] if name == "V" else ()
+            copies[(name, a, g, *tile)] = make(i, 0, 0, below(a, g), own_sem)
             if g == 2 or (g == 1 and a > 0):
-                to_next[a, g - 1].append(make(i, a, g - 1, below(0, 1), next_sem))
+                to_next[(name, a, g - 1, *tile)] = make(i, a, g - 1, below(0, 1), next_sem)
             if g == 2 and a > 0:
-                to_second[a, 0].append(make(i, a, 0, below(0, 2), second_sem))
-
-    def start(partner):
-        for copy in copies[partner]:
-            copy.start()
-
-    for a, g in PARTNERS:
-        when(
-            always(sends(a, g), jnp.logical_not(sends_over_end(a, g))),
-            lambda a=a, g=g: start((a, g)),
-        )
-    for a, g in PARTNERS:
-
-        @pl.when(always(sends(a, g), sends_over_end(a, g)))
-        def _():
-            pl.semaphore_wait(ready.at[PARTNERS.index((a, g))], 1)
-            start((a, g))
-
-    def each(some):
-        def start_all():
-            for copy in some:
-                copy.start()
-
-        return start_all
-
-    def arrived(g):
-        for a, slot_g in slots:
-            if slot_g == g:
-                for copy in copies[a, g]:
-                    copy.wait_recv()
-                onward = to_next[a, g]
-                when(odd if g == 1 else bool(onward), each(onward))
-                if to_second[a, g]:
-                    when(odd, each(to_second[a, g]))
+                to_second[(name, a, 0, *tile)] = make(i, a, 0, below(0, 2), second_sem)
+
+    def start(*partners):
+        for key in ORDER:
+            if key[1:3] in partners:
+                copies[key].start()
+
+    for key in ORDER:
+        a, g = key[1:3]
+        when(always(sends(a, g), jnp.logical_not(sends_over_end(a, g))), copies[key].start)
+
+    def send_over_end(*partners):
+        for a, g in partners:
+
+            @pl.when(always(sends(a, g), sends_over_end(a, g)))
+            def _():
+                pl.semaphore_wait(ready.at[PARTNERS.index((a, g))], 1)
+                start((a, g))
+
+    def take(*keys):
+        for key in keys:
+            copies[key].wait_recv()
+            if key in to_next:
+                when(odd if key[2] == 1 else True, to_next[key].start)
+            if key in to_second:
+                when(odd, to_second[key].start)
 
     def both_halves(a, g):
         value = load(edge, (a, g, 2), 2)
@@ -378,39 +378,26 @@
 
     loops = [(r, xp) for r in range(1, RMAX + 1) for xp in range(2)]
     last = [(r, xp) for r, xp in loops if xp + (r + 1) // 2 == 4]
-    arrived(0)
+    send_over_end((0, 1), (0, 2))
+    take(("V", 0, 1, 0), ("E", 1, 0), ("E", 2, 0))
+    send_over_end((1, 0), (2, 0))
+    take(("V", 1, 0, 0), ("E", 1, 1), ("E", 2, 1), ("V", 1, 0, 1))
     change_of_gauge(1)
     chains(0)
-    arrived(1)
+    take(("V", 1, 1, 0), ("V", 0, 1, 1), ("E", 0, 1), ("V", 1, 1, 1))
     chains(1)
     change_of_gauge(2)
     sums = correlate(zero, [loop for loop in loops if loop not in last])
-    arrived(2)
+    take(("E", 1, 2), ("E", 2, 2), ("V", 0, 2, 0), ("V", 1, 2, 0))
     chains(2)
     part[...] = correlate(sums, last)
 
-    for a, g in PARTNERS:
-
-        def sent(a=a, g=g):
-            for copy in copies[a, g]:
-                copy.wait_send()
-
-        when(sends(a, g), sent)
-
-    for slot in slots:
-
-        def relayed(some):
-            def wait_all():
-                for copy in some:
-                    copy.wait_send()
-
-            return wait_all
-
-        if to_next[slot]:
-            when(odd if slot[1] == 1 else True, relayed(to_next[slot]))
-        if to_second[slot]:
-            when(odd, relayed(to_second[slot]))
-
+    for key in ORDER:
+        when(sends(*key[1:3]), copies[key].wait_send)
+    for key, copy in to_next.items():
+        when(odd if key[2] == 1 else True, copy.wait_send)
+    for copy in to_second.values():
+        when(odd, copy.wait_send)
     swap = pltpu.make_async_remote_copy(
         src_ref=part,
         dst_ref=peer,

time: 23.5 us -> 25 us (1.064)
  the two profiles are of different devices: /device:TPU:227 before, /device:TPU:224 now
where the time goes in v4:
time: 25 us; the launch traced here: 24.8 us
  Pallas kernels  23.4 us (94%)
  local copies, waits for them, and re-layouts  1.42 us (6%)
    pallas_call x1, Pallas kernels, local(): pl.pallas_call(lambda *refs: kernel(sizes, *refs), out_shape=jax.ShapeDty...  23.4 us
    unnamed x1, local copies, waits for them, and re-layouts  1.42 us

profile of v4, /device:TPU:224, one launch (start us, length us, event | category | flops | bytes accessed | tf_op | source)
XLA Modules:
  0.0 24.8 jit_solution(13788336182238131413)
XLA Ops:
  0.0 23.4 %shard_map.28 = f32[6,4,4,6]{3,2,1,0:T(4,128)} custom-call(f32[18,16,128]{2,1,0:T(8,128)} %bitcast.4, f32[18,16,128]{2,1,0:T(8,128)} %bitcast.5), custom_call_target="tpu_custom_call" | custom-call | tf_op jit(solution)/shard_map/pallas_call | solution.py:429
  23.4 1.4 %copy.4 = f32[6,6,4,4]{1,3,2,0:T(4,128)} copy(f32[6,6,4,4]{1,3,2,0:T(4,128)} %bitcast.3) | data formatting | bytes 4608

commit v5 on v3

--- a/solution.py
+++ b/solution.py
@@ -441,7 +441,7 @@
         vmem = lambda *shape: pltpu.VMEM(shape, jnp.float32)
         sums = pl.pallas_call(
             lambda *refs: kernel(sizes, *refs),
-            out_shape=jax.ShapeDtypeStruct((RMAX, 4, 4, TMAX), jnp.float32),
+            out_shape=pltpu.VMEM((RMAX, 4, 4, TMAX), jnp.float32),
             in_specs=[pl.BlockSpec(memory_space=pl.ANY)] * 2,
             out_specs=pl.BlockSpec(memory_space=pltpu.VMEM),
             scratch_shapes=[

time: 23.5 us -> 22.1 us (0.940)
  local copies, waits for them, and re-layouts: 1.42 us -> 0.62 us
  Pallas kernels: 21.9 us -> 21.3 us
    unnamed x1, local copies, waits for them, and re-layouts: 1.42 us -> 0.62 us
    pallas_call x1, Pallas kernels: 21.9 us -> 21.3 us  [local(): pl.pallas_call(lambda *refs: kernel(sizes, *refs), out_shape=pltpu.VMEM((...]
where the time goes in v5:
time: 22.1 us; the launch traced here: 22 us
  Pallas kernels  21.3 us (96%)
  local copies, waits for them, and re-layouts  0.62 us (3%)
    pallas_call x1, Pallas kernels, local(): pl.pallas_call(lambda *refs: kernel(sizes, *refs), out_shape=pltpu.VMEM((...  21.3 us
    unnamed x1, local copies, waits for them, and re-layouts  0.62 us

profile of v5, /device:TPU:227, one launch (start us, length us, event | category | flops | bytes accessed | tf_op | source)
XLA Modules:
  0.0 22.0 jit_solution(761643947763969732)
XLA Ops:
  0.0 21.3 %shard_map.28 = f32[6,4,4,6]{3,2,1,0:T(4,128)S(1)} custom-call(f32[18,16,128]{2,1,0:T(8,128)} %bitcast.4, f32[18,16,128]{2,1,0:T(8,128)} %bitcast.5), custom_call_target="tpu_custom_call" | custom-call | tf_op jit(solution)/shard_map/pallas_call | solution.py:442
  21.3 0.6 %copy.4 = f32[6,6,4,4]{1,3,2,0:T(4,128)} copy(f32[6,6,4,4]{1,3,2,0:T(4,128)S(1)} %bitcast.3) | data formatting | bytes 4608

commit v6 on v4

--- a/solution.py
+++ b/solution.py
@@ -160,6 +160,27 @@
     copy_x.start()
     copy_t.start()
 
+    def enter():
+        @pl.when(peers > 0)
+        def _():
+            pl.semaphore_wait(barrier, peers)
+
+        for k, (a, g) in enumerate(PARTNERS):
+
+            @pl.when(always(receives(a, g), receives_over_end(a, g)))
+            def _():
+                pl.semaphore_signal(ready.at[k], inc=1, device_id=above(a, g), device_id_type=MESH)
+
+        @pl.when(y_at > 0)
+        def _():
+            pl.semaphore_signal(y_ready, inc=1, device_id={"gy": other_y}, device_id_type=MESH)
+
+    late = (t_at + 2 >= n_t) | (x_at + 2 >= n_x)
+
+    @pl.when(late)
+    def _():
+        enter()
+
     row = lax.broadcasted_iota(jnp.int32, (8, 128), 0)
     time = lax.rem(row, 4)
     lower = row < 4
@@ -201,19 +222,9 @@
     store(edge, (0, 0, 1), per_element(first_times, starts[0][:2], starts[1][:2]), 2)
 
 
-    @pl.when(peers > 0)
+    @pl.when(jnp.logical_not(late))
     def _():
-        pl.semaphore_wait(barrier, peers)
-
-    for k, (a, g) in enumerate(PARTNERS):
-
-        @pl.when(always(receives(a, g), receives_over_end(a, g)))
-        def _():
-            pl.semaphore_signal(ready.at[k], inc=1, device_id=above(a, g), device_id_type=MESH)
-
-    @pl.when(y_at > 0)
-    def _():
-        pl.semaphore_signal(y_ready, inc=1, device_id={"gy": other_y}, device_id_type=MESH)
+        enter()
 
     def v_copy(i, a, g, target, send_sem):
         to_a, to_g, pair = V_COPIES[i]
@@ -295,12 +306,12 @@
                 else:
                     value = matmul(value, both_halves(a, 1))
             if a == 2:
-                store(left, (2,), spread(value, 2, 0), 2)
-                store(right, (2,), spread(value, 3, 1), 3)
+                store(left, (g - 1, 2), spread(value, 2, 0), 2)
+                store(right, (g - 1, 2), spread(value, 3, 1), 3)
             else:
-                store(left, (a,), value[:2], 2)
+                store(left, (g - 1, a), value[:2], 2)
                 after = pick(time == 3, previous, rolled(value, 7))
-                store(right, (a,), after, 3)
+                store(right, (g - 1, a), after, 3)
             previous = spread(value, 3, 0)
 
     def row_pair(a, g, piece, q):
@@ -311,8 +322,8 @@
 
     def into_window(value, a, g):
         if g > 0:
-            value = third_row(matmul_dagger(value, load(right, (a,), 3)))
-            value = matmul(load(left, (a,), 2), value)
+            value = third_row(matmul_dagger(value, load(right, (g - 1, a), 3)))
+            value = matmul(load(left, (g - 1, a), 2), value)
         return third_row(value)
 
     def pair(g, q):
@@ -369,28 +380,36 @@
 
         return lax.fori_loop(0, TMAX, body, sums)
 
-    def chains(g):
+    def chains(g, first, end):
         def body(q, carry):
             pair(g, q)
             return carry
 
-        lax.fori_loop(0, 2 if g < 2 else 1, body, 0)
+        lax.fori_loop(first, end, body, 0)
 
     loops = [(r, xp) for r in range(1, RMAX + 1) for xp in range(2)]
-    last = [(r, xp) for r, xp in loops if xp + (r + 1) // 2 == 4]
+
+    def reaching(m):
+        return [(r, xp) for r, xp in loops if xp + (r + 1) // 2 == m]
+
     send_over_end((0, 1), (0, 2))
-    take(("V", 0, 1, 0), ("E", 1, 0), ("E", 2, 0))
-    send_over_end((1, 0), (2, 0))
-    take(("V", 1, 0, 0), ("E", 1, 1), ("E", 2, 1), ("V", 1, 0, 1))
+    take(("E", 1, 0), ("V", 1, 0, 0),)
+    send_over_end((2, 0), (1, 0))
+    take(("E", 2, 0), ("V", 1, 0, 1),)
     change_of_gauge(1)
-    chains(0)
-    take(("V", 1, 1, 0), ("V", 0, 1, 1), ("E", 0, 1), ("V", 1, 1, 1))
-    chains(1)
+    chains(0, 0, 2)
+    sums = correlate(zero, reaching(1))
+    take(("V", 0, 1, 0), ("E", 1, 1), ("E", 2, 1), ("V", 1, 1, 0))
+    chains(1, 0, 1)
+    sums = correlate(sums, reaching(2))
+    take(("E", 0, 1),)
     change_of_gauge(2)
-    sums = correlate(zero, [loop for loop in loops if loop not in last])
+    take(("V", 0, 1, 1), ("V", 1, 1, 1))
+    chains(1, 1, 2)
+    sums = correlate(sums, reaching(3))
     take(("E", 1, 2), ("E", 2, 2), ("V", 0, 2, 0), ("V", 1, 2, 0))
-    chains(2)
-    part[...] = correlate(sums, last)
+    chains(2, 0, 1)
+    part[...] = correlate(sums, reaching(4))
 
     for key in ORDER:
         when(sends(*key[1:3]), copies[key].wait_send)
@@ -428,7 +447,7 @@
         vmem = lambda *shape: pltpu.VMEM(shape, jnp.float32)
         sums = pl.pallas_call(
             lambda *refs: kernel(sizes, *refs),
-            out_shape=jax.ShapeDtypeStruct((RMAX, 4, 4, TMAX), jnp.float32),
+            out_shape=pltpu.VMEM((RMAX, 4, 4, TMAX), jnp.float32),
             in_specs=[pl.BlockSpec(memory_space=pl.ANY)] * 2,
             out_specs=pl.BlockSpec(memory_space=pltpu.VMEM),
             scratch_shapes=[
@@ -436,8 +455,8 @@
                 vmem(18, 16, 128),
                 vmem(2, 5, 12, 8, 128),
                 vmem(3, 3, 3, 12, 4, 128),
-                vmem(3, 12, 8, 128),
-                vmem(3, 18, 8, 128),
+                vmem(2, 3, 12, 8, 128),
+                vmem(2, 3, 18, 8, 128),
                 vmem(3, 18, 8, 128),
                 vmem(TMAX, 5, 18, 8, 128),
                 vmem(12, 8, 128),

time: 25 us -> 21.4 us (0.86)
  the two profiles are of different devices: /device:TPU:224 before, /device:TPU:227 now
where the time goes in v6:
time: 21.4 us; the launch traced here: 21.3 us
  Pallas kernels  20.6 us (96%)
  local copies, waits for them, and re-layouts  0.62 us (3%)
    pallas_call x1, Pallas kernels, local(): pl.pallas_call(lambda *refs: kernel(sizes, *refs), out_shape=pltpu.VMEM((...  20.6 us
    unnamed x1, local copies, waits for them, and re-layouts  0.62 us

profile of v6, /device:TPU:227, one launch (start us, length us, event | category | flops | bytes accessed | tf_op | source)
XLA Modules:
  0.0 21.3 jit_solution(13416138100234051645)
XLA Ops:
  0.0 20.6 %shard_map.28 = f32[6,4,4,6]{3,2,1,0:T(4,128)S(1)} custom-call(f32[18,16,128]{2,1,0:T(8,128)} %bitcast.4, f32[18,16,128]{2,1,0:T(8,128)} %bitcast.5), custom_call_target="tpu_custom_call" | custom-call | tf_op jit(solution)/shard_map/pallas_call | solution.py:448
  20.7 0.6 %copy.4 = f32[6,6,4,4]{1,3,2,0:T(4,128)} copy(f32[6,6,4,4]{1,3,2,0:T(4,128)S(1)} %bitcast.3) | data formatting | bytes 4608

commit v7 on v6

--- a/solution.py
+++ b/solution.py
@@ -406,17 +406,10 @@
     change_of_gauge(2)
     take(("V", 0, 1, 1), ("V", 1, 1, 1))
     chains(1, 1, 2)
-    sums = correlate(sums, reaching(3))
     take(("E", 1, 2), ("E", 2, 2), ("V", 0, 2, 0), ("V", 1, 2, 0))
     chains(2, 0, 1)
-    part[...] = correlate(sums, reaching(4))
-
-    for key in ORDER:
-        when(sends(*key[1:3]), copies[key].wait_send)
-    for key, copy in to_next.items():
-        when(odd if key[2] == 1 else True, copy.wait_send)
-    for copy in to_second.values():
-        when(odd, copy.wait_send)
+    part[...] = correlate(sums, reaching(3) + reaching(4))
+
     swap = pltpu.make_async_remote_copy(
         src_ref=part,
         dst_ref=peer,
@@ -431,6 +424,12 @@
         pl.semaphore_wait(y_ready, 1)
 
     swap.start()
+    for key in ORDER:
+        when(sends(*key[1:3]), copies[key].wait_send)
+    for key, copy in to_next.items():
+        when(odd if key[2] == 1 else True, copy.wait_send)
+    for copy in to_second.values():
+        when(odd, copy.wait_send)
     swap.wait()
     sums = (part[...] + peer[...]) / (3.0 * 128 * n_y)
     for r, xp in loops:

time: 21.4 us -> 21.1 us (0.986)
  Pallas kernels: 20.6 us -> 20.3 us
    pallas_call x1, Pallas kernels: 20.6 us -> 20.3 us  [local(): pl.pallas_call(lambda *refs: kernel(sizes, *refs), out_shape=pltpu.VMEM((...]
where the time goes in v7:
time: 21.1 us; the launch traced here: 21 us
  Pallas kernels  20.3 us (96%)
  local copies, waits for them, and re-layouts  0.62 us (3%)
    pallas_call x1, Pallas kernels, local(): pl.pallas_call(lambda *refs: kernel(sizes, *refs), out_shape=pltpu.VMEM((...  20.3 us
    unnamed x1, local copies, waits for them, and re-layouts  0.62 us

profile of v7, /device:TPU:227, one launch (start us, length us, event | category | flops | bytes accessed | tf_op | source)
XLA Modules:
  0.0 21.0 jit_solution(9988297631119984195)
XLA Ops:
  0.0 20.3 %shard_map.28 = f32[6,4,4,6]{3,2,1,0:T(4,128)S(1)} custom-call(f32[18,16,128]{2,1,0:T(8,128)} %bitcast.4, f32[18,16,128]{2,1,0:T(8,128)} %bitcast.5), custom_call_target="tpu_custom_call" | custom-call | tf_op jit(solution)/shard_map/pallas_call | solution.py:447
  20.3 0.6 %copy.4 = f32[6,6,4,4]{1,3,2,0:T(4,128)} copy(f32[6,6,4,4]{1,3,2,0:T(4,128)S(1)} %bitcast.3) | data formatting | bytes 4608

commit v8 on v7

--- a/solution.py
+++ b/solution.py
@@ -393,17 +393,18 @@
         return [(r, xp) for r, xp in loops if xp + (r + 1) // 2 == m]
 
     send_over_end((0, 1), (0, 2))
-    take(("E", 1, 0), ("V", 1, 0, 0),)
+    take(("E", 1, 0), ("V", 1, 0, 0))
     send_over_end((2, 0), (1, 0))
-    take(("E", 2, 0), ("V", 1, 0, 1),)
+    take(("E", 2, 0),)
     change_of_gauge(1)
+    take(("V", 1, 0, 1),)
     chains(0, 0, 2)
     sums = correlate(zero, reaching(1))
-    take(("V", 0, 1, 0), ("E", 1, 1), ("E", 2, 1), ("V", 1, 1, 0))
+    take(("V", 0, 1, 0), ("E", 1, 1), ("E", 2, 1), ("E", 0, 1))
+    change_of_gauge(2)
+    take(("V", 1, 1, 0),)
     chains(1, 0, 1)
     sums = correlate(sums, reaching(2))
-    take(("E", 0, 1),)
-    change_of_gauge(2)
     take(("V", 0, 1, 1), ("V", 1, 1, 1))
     chains(1, 1, 2)
     take(("E", 1, 2), ("E", 2, 2), ("V", 0, 2, 0), ("V", 1, 2, 0))

time: 21.1 us -> 20.9 us (level)
    pallas_call x1, Pallas kernels: 20.3 us -> 20.1 us  [local(): pl.pallas_call(lambda *refs: kernel(sizes, *refs), out_shape=pltpu.VMEM((...]
where the time goes in v8:
time: 20.9 us; the launch traced here: 20.8 us
  Pallas kernels  20.1 us (96%)
  local copies, waits for them, and re-layouts  0.62 us (3%)
    pallas_call x1, Pallas kernels, local(): pl.pallas_call(lambda *refs: kernel(sizes, *refs), out_shape=pltpu.VMEM((...  20.1 us
    unnamed x1, local copies, waits for them, and re-layouts  0.62 us

profile of v8, /device:TPU:227, one launch (start us, length us, event | category | flops | bytes accessed | tf_op | source)
XLA Modules:
  0.0 20.8 jit_solution(9478020320254479809)
XLA Ops:
  0.0 20.1 %shard_map.28 = f32[6,4,4,6]{3,2,1,0:T(4,128)S(1)} custom-call(f32[18,16,128]{2,1,0:T(8,128)} %bitcast.4, f32[18,16,128]{2,1,0:T(8,128)} %bitcast.5), custom_call_target="tpu_custom_call" | custom-call | tf_op jit(solution)/shard_map/pallas_call | solution.py:448
  20.1 0.6 %copy.4 = f32[6,6,4,4]{1,3,2,0:T(4,128)} copy(f32[6,6,4,4]{1,3,2,0:T(4,128)S(1)} %bitcast.3) | data formatting | bytes 4608
